TPU v7x, 32 devices: a whole 2x2x4 slice. The times are simulated.
32 devices in a mesh: groups: 2 (over y), seq: 4 (over z), slide: 2 (over x), head: 2 (over core).
Axes of the slice: x: 2, y: 2, z: 4, core: 2. Of those that a mesh axis runs over, the one named last changes fastest.
Arguments:
- latents: bfloat16 [1024, 1024], P(('groups', 'seq'), 'head'), parts along dimension 0, may hold values from -153 to 153
- tile_keys: bfloat16 [4, 1024, 1024], P(('groups', 'slide'), 'seq', 'head'), parts along dimension 0, may hold values from -6 to 6
- tile_values: bfloat16 [4, 1024, 1024], P(('groups', 'slide'), 'seq', 'head'), parts along dimension 0, may hold values from -24 to 24
- tile_mask: int32 [4, 8], P(('groups', 'slide'), 'seq'), parts along dimension 0, may hold values from 0 to 1, as said below
- latent_counts: int32 [4], P(('groups', 'slide')), parts along dimension 0, may hold values from 128 to 512
- out_weight: bfloat16 [1024, 1024], P('head'), may hold values from -0.1875 to 0.1875
- cotangent: bfloat16 [4, 512, 1024], P(('groups', 'slide'), 'seq'), parts along dimension 0, may hold values from -6 to 6
Outputs:
- pooled: bfloat16 [4, 512, 1024], P(('groups', 'slide'), 'seq', 'head'), parts along dimension 0
- grad_latents: float32 [1024, 1024], P(('groups', 'seq'), 'head'), parts along dimension 0
- grad_keys: bfloat16 [4, 1024, 1024], P(('groups', 'slide'), 'seq', 'head'), parts along dimension 0
- grad_values: bfloat16 [4, 1024, 1024], P(('groups', 'slide'), 'seq', 'head'), parts along dimension 0
There are 2 independent parts, one for each index of `groups`. A program takes and returns all parts, laid end to end along the dimension named above; an argument that names none is the same for every part. Nothing has to cross between parts.
Inputs may be any that keep to these rules, and one draw needn't show every extreme that they name: `tile_mask`: every slide has at least one block of 128 tiles marked 1.
All inputs are finite; a program needn't handle non-finite values.
Results may differ from a plain program's by a relative error of at most 0.035.
Values may be sent and summed in bfloat16 or wider, within the bound.
No kernel may reach another device: no remote copies, remote signals or barrier semaphores. Data moves between devices by JAX's collectives and lax.ppermute only.
A program may use at most 64 MiB of HBM per device.

v0:
```python
import jax
import jax.numpy as jnp
from jax import lax
from jax.sharding import PartitionSpec as P

HD = 64
BLOCK = 128
masked_score = -1e30


def body(latents, tile_keys, tile_values, tile_mask, latent_counts, out_weight, cotangent):
    local_rows = latents.shape[0]
    local_width = latents.shape[1]
    head_count = local_width // HD
    factor = HD ** (-0.5)
    queries = lax.all_gather(latents, "seq", axis=0, tiled=True)
    total_rows = queries.shape[0]
    first_row = lax.axis_index("seq") * local_rows
    every_row = lax.broadcasted_iota(jnp.int32, (total_rows, 1), 0)
    own_row = lax.broadcasted_iota(jnp.int32, (local_rows, 1), 0) + first_row
    tile_count = tile_keys.shape[1]
    key_block = tile_keys[0]
    value_block = tile_values[0]
    valid_tiles = jnp.broadcast_to(tile_mask[0][:, None] > 0, (tile_count // BLOCK, BLOCK)).reshape(
        1, tile_count
    )
    live_count = latent_counts[0]
    score_list = []
    for which_head in range(head_count):
        columns = slice(which_head * HD, (which_head + 1) * HD)
        raw_scores = (
            jnp.einsum(
                "qc,tc->qt",
                queries[:, columns],
                key_block[:, columns],
                preferred_element_type=jnp.float32,
            )
            * factor
        )
        score_list.append(jnp.where(valid_tiles, raw_scores, masked_score))
    local_top = jnp.stack([jnp.max(scored, axis=1) for scored in score_list], axis=1)
    row_top = lax.pmax(local_top, "seq")
    expo_list = []
    weighted_list = []
    total_list = []
    for which_head in range(head_count):
        columns = slice(which_head * HD, (which_head + 1) * HD)
        expos = jnp.where(
            valid_tiles,
            jnp.exp(score_list[which_head] - row_top[:, which_head : which_head + 1]),
            0.0,
        )
        expo_list.append(expos)
        total_list.append(jnp.sum(expos, axis=1))
        weighted_list.append(
            jnp.dot(
                expos.astype(jnp.bfloat16),
                value_block[:, columns],
                preferred_element_type=jnp.float32,
            )
        )
    partial_sums = jnp.concatenate(weighted_list, axis=1)
    partial_totals = jnp.stack(total_list, axis=1)
    weighted, totals = lax.psum((partial_sums, partial_totals), "seq")
    span = weighted.shape[0]
    attended = jnp.where(
        every_row < live_count,
        (weighted.reshape(span, head_count, HD) / totals[:, :, None]).reshape(span, local_width),
        0.0,
    ).astype(jnp.bfloat16)
    own_attended = lax.dynamic_slice_in_dim(attended, first_row, local_rows, 0)
    pooled_part = jnp.dot(own_attended, out_weight, preferred_element_type=jnp.float32)
    pooled_parts = [
        lax.psum_scatter(pooled_part.astype(jnp.bfloat16), "head", scatter_dimension=1, tiled=True)
    ]
    projected = jnp.einsum(
        "rd,cd->rc", cotangent[0], out_weight, preferred_element_type=jnp.float32
    )
    upstream = jnp.where(own_row < live_count, projected, 0.0).astype(jnp.bfloat16)
    upstream_all = lax.all_gather(upstream, "seq", axis=0, tiled=True)
    row_delta = jnp.sum(
        (upstream_all.astype(jnp.float32) * attended.astype(jnp.float32)).reshape(
            total_rows, head_count, HD
        ),
        axis=2,
    )
    query_list = []
    key_list = []
    value_list = []
    for which_head in range(head_count):
        columns = slice(which_head * HD, (which_head + 1) * HD)
        up_head = upstream_all[:, columns]
        weights = expo_list[which_head] / totals[:, which_head : which_head + 1]
        value_list.append(
            jnp.einsum(
                "qt,qc->tc",
                weights.astype(jnp.bfloat16),
                up_head,
                preferred_element_type=jnp.float32,
            )
        )
        grad_prob = jnp.einsum(
            "qc,tc->qt", up_head, value_block[:, columns], preferred_element_type=jnp.float32
        )
        grad_score = (
            weights * (grad_prob - row_delta[:, which_head : which_head + 1]) * factor
        ).astype(jnp.bfloat16)
        query_list.append(
            jnp.dot(grad_score, key_block[:, columns], preferred_element_type=jnp.float32)
        )
        key_list.append(
            jnp.einsum(
                "qt,qc->tc", grad_score, queries[:, columns], preferred_element_type=jnp.float32
            )
        )
    grad_rows = jnp.concatenate(query_list, axis=1)
    key_grads = [jnp.concatenate(key_list, axis=1).astype(jnp.bfloat16)]
    value_grads = [jnp.concatenate(value_list, axis=1).astype(jnp.bfloat16)]
    own_grad = lax.psum_scatter(
        grad_rows.astype(jnp.bfloat16), "seq", scatter_dimension=0, tiled=True
    )
    grad_latents = lax.psum(own_grad, "slide").astype(jnp.float32)
    return (
        jnp.stack(pooled_parts, axis=0),
        grad_latents,
        jnp.stack(key_grads, axis=0),
        jnp.stack(value_grads, axis=0),
    )


def solution(mesh):
    placed = (
        P(("groups", "seq"), "head"),
        P(("groups", "slide"), "seq", "head"),
        P(("groups", "slide"), "seq", "head"),
        P(("groups", "slide"), "seq"),
        P(("groups", "slide")),
        P("head", None),
        P(("groups", "slide"), "seq", None),
    )
    return jax.shard_map(
        body,
        mesh=mesh,
        in_specs=placed,
        out_specs=(
            P(("groups", "slide"), "seq", "head"),
            P(("groups", "seq"), "head"),
            P(("groups", "slide"), "seq", "head"),
            P(("groups", "slide"), "seq", "head"),
        ),
        check_vma=False,
    )
```

profile of v0, /device:TPU:0, one launch (start us, length us, event | category | flops | bytes accessed | tf_op | source)
XLA Modules:
  0.0 189.9 jit_solution(3926986250691564147)
XLA Ops:
  8.0 17.7 %all_gather.6 = bf16[512,512]{1,0:T(8,128)(2,1)S(1)} all-gather(bf16[128,512]{1,0:T(8,128)(2,1)} %param.7), channel_id=1, replica_groups=mesh['groups'=2,'seq'=4,'slide'=2,'head'=2] {'seq'}, dimensions={0}, use_global_device_ids=true | all-gather | bytes 655360 | tf_op jit(solution)/shard_map/all_gather | solution.py:16
  26.6 1.0 fusion.230
  27.7 1.1 fusion.229
  28.8 1.1 fusion.228
  29.8 1.1 fusion.227
  30.9 1.1 fusion.226
  32.0 19.5 %pmax.7 = f32[512,8]{0,1:T(8,128)S(1)} all-reduce(f32[512,8]{0,1:T(8,128)S(1)} %stack.67), channel_id=1, replica_groups=mesh['groups'=2,'seq'=4,'slide'=2,'head'=2] {'seq'}, use_global_device_ids=true, to_apply=%region_8.9 | all-reduce | flops 4096 | bytes 32768 | tf_op jit(solution)/shard_map/pmax | solution.py:42
  51.6 2.0 %convolution_dynamic-update-slice_fusion.7 = f32[512,512]{0,1:T(8,128)} fusion(f32[512,256]{0,1:T(8,128)} %get-tuple-element.51, f32[512]{0:T(512)S(1)} %bitcast.205, pred[256]{0:T(512)(128)(4,1)S(1)} %broadcast_bitcast_fusion, bf16[256,512]{1,0:T(8,128)(2,1)S(1)} %bitcast.161), kind=kOutput, calls=%fused_computation.57 | convolution fusion | flops 17170432 | bytes 723456 | tf_op jit(solution)/shard_map/dot_general | solution.py:56
  53.6 0.9 convolution_dynamic-update-slice_fusion.6
  54.6 0.9 convolution_dynamic-update-slice_fusion.5
  55.6 0.9 convolution_dynamic-update-slice_fusion.4
  56.6 0.9 convolution_dynamic-update-slice_fusion.3
  57.5 0.9 convolution_dynamic-update-slice_fusion.2
  58.5 0.9 convolution_dynamic-update-slice_fusion.1
  59.4 0.9 convolution_dynamic-update-slice_fusion
  60.4 2.5 %fusion.97 = (f32[512]{0:T(512)S(1)}, f32[512]{0:T(512)S(1)}, f32[512]{0:T(512)S(1)}, f32[512]{0:T(512)S(1)}, f32[512]{0:T(512)S(1)}, /*index=5*/f32[512]{0:T(512)S(1)}, f32[512]{0:T(512)S(1)}, f32[512]{0:T(512)S(1)}) fusion(f32[512,256]{0,1:T(8,128)S(1)} %get-tuple-element.65, f32[512]{0:T(512)S(1)} %bitcast.182, ...), kind=kLoop, calls=%fused_computation.158 | loop fusion | flops 3141632 | bytes 4227328 | tf_op jit(solution)/shard_map/reduce_sum | solution.py:54
  63.5 1.4 fusion.32
  64.9 21.1 %all_gather.7 = bf16[512,512]{0,1:T(8,128)(2,1)S(1)} all-gather(bf16[128,512]{0,1:T(8,128)(2,1)S(1)} %fusion.32), channel_id=1, replica_groups=mesh['groups'=2,'seq'=4,'slide'=2,'head'=2] {'seq'}, dimensions={0}, use_global_device_ids=true | all-gather | bytes 655360 | tf_op jit(solution)/shard_map/all_gather | solution.py:80
  86.0 19.5 %psum.22 = f32[512,8]{0,1:T(8,128)S(1)} all-reduce(f32[512,8]{0,1:T(8,128)S(1)} %stack.76), channel_id=1, replica_groups=mesh['groups'=2,'seq'=4,'slide'=2,'head'=2] {'seq'}, use_global_device_ids=true, to_apply=%region_18.19 | all-reduce | flops 4096 | bytes 32768 | tf_op jit(solution)/shard_map/psum | solution.py:64
  105.6 2.0 %fusion.42 = bf16[1,256,512]{1,2,0:T(8,128)(2,1)} fusion(bf16[512,512]{0,1:T(8,128)(2,1)S(1)} %all_gather.7, f32[512,256]{0,1:T(8,128)} %get-tuple-element.51, f32[512]{0:T(512)S(1)} %bitcast.231, f32[512]{0:T(512)S(1)} %bitcast.207, pred[256]{0:T(512)(128)(4,1)S(1)} %broadcast_bitcast_fusion), kind=kOutput, calls=%fused_computation.92 | convolution fusion | flops 17317888 | bytes 627200 | tf_op jit(solution)/shard_map/qt,qc->tc/dot_general | solution.py:95
  107.6 0.9 fusion.44
  108.7 0.9 fusion.46
  109.7 0.9 fusion.48
  114.5 1.8 copy.46
  116.3 2.3 %bitcast_reduce_fusion = (f32[512,8]{0,1:T(8,128)S(1)}, bf16[512,512]{0,1:T(8,128)(2,1)}) fusion(bf16[512,512]{0,1:T(8,128)(2,1)S(1)} %all_gather.7, f32[512,512]{0,1:T(8,128)} %all-reduce.3.cloned.1.call-done, f32[512,8]{0,1:T(8,128)S(1)} %psum.22, pred[512]{0:T(512)(128)(4,1)S(1)} %iota_compare_fusion), kind=kLoop, calls=%fused_computation.123 | loop fusion | flops 1830912 | bytes 2130432 | tf_op jit(solution)/shard_map/reduce_sum | solution.py:81
  128.0 1.0 copy.56
  133.1 2.0 %convolution_convert_fusion = bf16[128,1024]{1,0:T(8,128)(2,1)} fusion(bf16[512,1024]{1,0:T(8,128)(2,1)S(1)} %copy-done, bf16[512,512]{0,1:T(8,128)(2,1)} %get-tuple-element.25, s32[]{:T(128)S(6)} %select_n.77), kind=kOutput, calls=%fused_computation.48 | convolution fusion | flops 134348800 | bytes 1441796 | tf_op jit(solution)/shard_map/dot_general | solution.py:72
  135.1 15.1 %reduce-scatter.7.cloned.1.call-done = bf16[128,512]{1,0:T(8,128)(2,1)} async-done(((bf16[512,512]{1,0:T(8,128)(2,1)}), bf16[128,512]{1,0:T(8,128)(2,1)}) %reduce-scatter.7.cloned.1.call-update) | async-done | bytes 131088
  150.2 1.7 copy.57
  154.5 18.5 %all-reduce.5.cloned.1.call-done = bf16[128,512]{0,1:T(8,128)(2,1)} async-done(((bf16[128,512]{0,1:T(8,128)(2,1)}), bf16[128,512]{0,1:T(8,128)(2,1)}) %all-reduce.5.cloned.1.call-update) | async-done | bytes 131088 | tf_op jit(solution)/shard_map/psum | solution.py:122
  173.0 1.7 copy.44
  174.7 8.7 %reduce-scatter.5.cloned.1.call-done = bf16[128,512]{1,0:T(8,128)(2,1)} async-done(((bf16[128,1024]{1,0:T(8,128)(2,1)}), bf16[128,512]{1,0:T(8,128)(2,1)}) %reduce-scatter.5.cloned.1.call-update) | async-done | bytes 131088 | tf_op jit(solution)/shard_map/reduce_scatter | solution.py:74
  (120 shorter events, 22.2 us)
Async XLA Ops:
  7.2 56.3 %copy-start = (bf16[512,1024]{1,0:T(8,128)(2,1)S(1)}, bf16[512,1024]{1,0:T(8,128)(2,1)}, u32[]{:S(2)}) copy-start(bf16[512,1024]{1,0:T(8,128)(2,1)} %param.12) | copy-start | bytes 3145732
  7.2 109.1 %all-reduce.3.cloned.1.call-start = ((), (), s32[]{:S(2)}) async-start(), calls=%async_computation.2 | async-start | bytes 2097152 | tf_op jit(solution)/shard_map/psum | solution.py:64
  8.0 17.7 %copy-start.28 = (bf16[1,256,512]{2,1,0:T(8,128)(2,1)S(1)}, bf16[1,256,512]{2,1,0:T(8,128)(2,1)}, u32[]{:S(2)}) copy-start(bf16[1,256,512]{2,1,0:T(8,128)(2,1)} %param.8) | copy-start | bytes 786436
  26.6 33.7 %copy-start.1 = (f32[512,256]{0,1:T(8,128)}, f32[512,256]{0,1:T(8,128)S(1)}, u32[]{:S(2)}) copy-start(f32[512,256]{0,1:T(8,128)S(1)} %get-tuple-element.61) | copy-start | bytes 1572868
  30.9 20.6 %copy-start.30 = (bf16[1,256,512]{2,1,0:T(8,128)(2,1)S(1)}, bf16[1,256,512]{2,1,0:T(8,128)(2,1)}, u32[]{:S(2)}) copy-start(bf16[1,256,512]{2,1,0:T(8,128)(2,1)} %param.9) | copy-start | bytes 786436
  51.6 2.0 %copy-start.13 = (f32[512,256]{0,1:T(8,128)S(1)}, f32[512,256]{0,1:T(8,128)}, u32[]{:S(2)}) copy-start(f32[512,256]{0,1:T(8,128)} %get-tuple-element.53) | copy-start | bytes 1572868
  53.6 1.0 copy-start.10
  54.5 1.1 copy-start.7
  55.6 1.1 copy-start.4
  60.3 89.9 %reduce-scatter.7.cloned.1.call-start = ((), (), s32[]{:S(2)}) async-start(), calls=%async_computation.5 | async-start | bytes 655360
  105.6 2.0 %copy-start.14 = (f32[512,256]{0,1:T(8,128)S(1)}, f32[512,256]{0,1:T(8,128)}, u32[]{:S(2)}) copy-start(f32[512,256]{0,1:T(8,128)} %get-tuple-element.53) | copy-start | bytes 1572868
  107.6 1.0 copy-start.11
  108.7 1.0 copy-start.8
  109.7 1.0 copy-start.5
  110.7 1.0 copy-start.2
  116.3 2.3 %copy-start.32 = (f32[512,256]{0,1:T(8,128)S(1)}, f32[512,256]{0,1:T(8,128)}, u32[]{:S(2)}) copy-start(f32[512,256]{0,1:T(8,128)} %get-tuple-element.51) | copy-start | bytes 1572868
  118.6 1.0 copy-start.15
  118.9 6.5 %copy-start.20 = (bf16[512,256]{0,1:T(8,128)(2,1)}, bf16[512,256]{0,1:T(8,128)(2,1)S(1)}, u32[]{:S(2)}) copy-start(bf16[512,256]{0,1:T(8,128)(2,1)S(1)} %fusion.31) | copy-start | bytes 786436
  119.7 1.0 copy-start.12
  120.0 6.3 %copy-start.22 = (bf16[512,256]{0,1:T(8,128)(2,1)}, bf16[512,256]{0,1:T(8,128)(2,1)S(1)}, u32[]{:S(2)}) copy-start(bf16[512,256]{0,1:T(8,128)(2,1)S(1)} %fusion.30) | copy-start | bytes 786436
  120.7 1.0 copy-start.9
  121.0 5.6 %copy-start.24 = (bf16[512,256]{0,1:T(8,128)(2,1)}, bf16[512,256]{0,1:T(8,128)(2,1)S(1)}, u32[]{:S(2)}) copy-start(bf16[512,256]{0,1:T(8,128)(2,1)S(1)} %fusion.29) | copy-start | bytes 786436
  121.8 1.0 copy-start.6
  122.1 4.7 %copy-start.26 = (bf16[512,256]{0,1:T(8,128)(2,1)}, bf16[512,256]{0,1:T(8,128)(2,1)S(1)}, u32[]{:S(2)}) copy-start(bf16[512,256]{0,1:T(8,128)(2,1)S(1)} %fusion.28) | copy-start | bytes 786436
  122.8 1.0 copy-start.3
  123.0 4.0 %copy-start.18 = (bf16[512,256]{0,1:T(8,128)(2,1)}, bf16[512,256]{0,1:T(8,128)(2,1)S(1)}, u32[]{:S(2)}) copy-start(bf16[512,256]{0,1:T(8,128)(2,1)S(1)} %fusion.27) | copy-start | bytes 786436
  124.1 3.1 %copy-start.16 = (bf16[512,256]{0,1:T(8,128)(2,1)}, bf16[512,256]{0,1:T(8,128)(2,1)S(1)}, u32[]{:S(2)}) copy-start(bf16[512,256]{0,1:T(8,128)(2,1)S(1)} %fusion.26) | copy-start | bytes 786436
  129.1 1.1 copy-start.23
  129.1 43.9 %all-reduce.5.cloned.1.call-start = ((), (), s32[]{:S(2)}) async-start(), calls=%async_computation.4 | async-start | bytes 262144 | tf_op jit(solution)/shard_map/psum | solution.py:122
  133.1 18.9 %copy-start.34 = (bf16[1,256,512]{1,2,0:T(8,128)(2,1)S(1)}, bf16[1,256,512]{1,2,0:T(8,128)(2,1)}, u32[]{:S(2)}) copy-start(bf16[1,256,512]{1,2,0:T(8,128)(2,1)} %copy-done.33) | copy-start | bytes 786436
  135.1 16.9 %copy-start.19 = (bf16[512,256]{0,1:T(8,128)(2,1)S(1)}, bf16[512,256]{0,1:T(8,128)(2,1)}, u32[]{:S(2)}) copy-start(bf16[512,256]{0,1:T(8,128)(2,1)} %copy-done.18) | copy-start | bytes 786436
  151.9 31.4 %reduce-scatter.5.cloned.1.call-start = ((), (), s32[]{:S(2)}) async-start(), calls=%async_computation.3 | async-start | bytes 393216 | tf_op jit(solution)/shard_map/reduce_scatter | solution.py:74
  (7 other events, 6.4 us)
Sparse Core Ops, SparseCore 0:
  60.4 55.6 all-reduce.2
  129.2 20.9 reduce-scatter.6
  153.1 19.8 all-reduce.4
  175.6 7.7 reduce-scatter.4
where the time goes:
time: 191 us; the launch traced here: 190 us
  blocking collectives  77.8 us (41%)
  waiting for transfers between devices  42.7 us (22%)
  matrix products  32.4 us (17%)
  local copies, waits for them, and re-layouts  16.6 us (9%)
  between operations  14.8 us (8%)
  other arithmetic  5.53 us (3%)
    all_gather x1, blocking collectives, body(): upstream_all = lax.all_gather(upstream, 'seq', axis=0, tiled=True)  21.1 us
    psum x1, blocking collectives, body(): weighted, totals = lax.psum((partial_sums, partial_totals), 'seq')  19.5 us
    pmax x1, blocking collectives, body(): row_top = lax.pmax(local_top, 'seq')  19.5 us
    psum x1, waiting for transfers between devices, body(): grad_latents = lax.psum(own_grad, 'slide').astype(jnp.float32)  18.5 us
    all_gather x1, blocking collectives, body(): queries = lax.all_gather(latents, 'seq', axis=0, tiled=True)  17.7 us
    unnamed x75, local copies, waits for them, and re-layouts  16.4 us
    unnamed x5, waiting for transfers between devices  15.5 us
    reduce_scatter x1, waiting for transfers between devices, body(): lax.psum_scatter(pooled_part.astype(jnp.bfloat16), 'head', scatter_dimens...  8.71 us
  transfers between devices with their start and end apart: 4, of which 3 were waited for; matrix products, arithmetic and copies ran while one was open for 11% of the time, Pallas kernels for 0%

commit v1 on v0

--- a/solution.py
+++ b/solution.py
@@ -6,6 +6,11 @@
 HD = 64
 BLOCK = 128
 masked_score = -1e30
+
+
+def carry_the_sectors(xin, which_axis):
+    val = lax.all_gather(xin, axis_name=which_axis)
+    return jnp.sum(val, axis=0)
 
 
 def body(latents, tile_keys, tile_values, tile_mask, latent_counts, out_weight, cotangent):
@@ -119,7 +124,7 @@
     own_grad = lax.psum_scatter(
         grad_rows.astype(jnp.bfloat16), "seq", scatter_dimension=0, tiled=True
     )
-    grad_latents = lax.psum(own_grad, "slide").astype(jnp.float32)
+    grad_latents = carry_the_sectors(own_grad, "slide").astype(jnp.float32)
     return (
         jnp.stack(pooled_parts, axis=0),
         grad_latents,

time: 191 us -> 172 us (0.901)
  waiting for transfers between devices: 42.7 us -> 15.1 us
  matrix products: 32.4 us -> 38.6 us
  blocking collectives: 77.8 us -> 83.5 us
  local copies, waits for them, and re-layouts: 16.6 us -> 13.1 us
    psum x1 -> x0, waiting for transfers between devices: 18.5 us -> none  [body(): grad_latents = lax.psum(own_grad, 'slide').astype(jnp.float32)]
    reduce_scatter x1, waiting for transfers between devices: 8.71 us -> 0.58 us  [body(): lax.psum_scatter(pooled_part.astype(jnp.bfloat16), 'head', scatter_dimens...]
    all_gather x0 -> x1, blocking collectives: none -> 5.67 us  [carry_the_sectors(): val = lax.all_gather(xin, axis_name=which_axis)]
    dot_general x8, matrix products: 1.97 us -> 6.92 us  [body(): jnp.dot(grad_score, key_block[:, columns], preferred_element_type=jnp.flo...]
    unnamed x75 -> x65, local copies, waits for them, and re-layouts: 16.4 us -> 12.8 us
    unnamed x5 -> x4, waiting for transfers between devices: 15.5 us -> 14.5 us
  transfers between devices with their start and end apart: 4 -> 3, of which waited for: 3 -> 2; matrix products, arithmetic and copies ran while one was open for 11% -> 12% of each run, Pallas kernels for 0% -> 0%
where the time goes in v1:
time: 172 us; the launch traced here: 171 us
  blocking collectives  83.5 us (49%)
  matrix products  38.6 us (22%)
  waiting for transfers between devices  15.1 us (9%)
  between operations  14.7 us (9%)
  local copies, waits for them, and re-layouts  13.1 us (8%)
  other arithmetic  6.22 us (4%)
    all_gather x1, blocking collectives, body(): upstream_all = lax.all_gather(upstream, 'seq', axis=0, tiled=True)  21.1 us
    psum x1, blocking collectives, body(): weighted, totals = lax.psum((partial_sums, partial_totals), 'seq')  19.5 us
    pmax x1, blocking collectives, body(): row_top = lax.pmax(local_top, 'seq')  19.5 us
    all_gather x1, blocking collectives, body(): queries = lax.all_gather(latents, 'seq', axis=0, tiled=True)  17.7 us
    unnamed x4, waiting for transfers between devices  14.5 us
    unnamed x65, local copies, waits for them, and re-layouts  12.8 us
    dot_general x8, matrix products, body(): jnp.dot(expos.astype(jnp.bfloat16), value_block[:, columns], preferred_el...  8.48 us
    dot_general x8, matrix products, body(): jnp.einsum('qt,qc->tc', weights.astype(jnp.bfloat16), up_head, preferred_...  8.28 us
  transfers between devices with their start and end apart: 3, of which 2 were waited for; matrix products, arithmetic and copies ran while one was open for 12% of the time, Pallas kernels for 0%

profile of v1, /device:TPU:0, one launch (start us, length us, event | category | flops | bytes accessed | tf_op | source)
XLA Modules:
  0.0 171.3 jit_solution(5143626990957413334)
XLA Ops:
  8.0 17.7 %all_gather.12 = bf16[512,512]{1,0:T(8,128)(2,1)S(1)} all-gather(bf16[128,512]{1,0:T(8,128)(2,1)} %param.7), channel_id=1, replica_groups=mesh['groups'=2,'seq'=4,'slide'=2,'head'=2] {'seq'}, dimensions={0}, use_global_device_ids=true | all-gather | bytes 655360 | tf_op jit(solution)/shard_map/all_gather | solution.py:21
  26.6 1.0 fusion.230
  27.7 1.1 fusion.229
  28.8 1.1 fusion.228
  29.8 1.1 fusion.227
  30.9 1.1 fusion.226
  32.0 19.5 %pmax.7 = f32[512,8]{0,1:T(8,128)S(1)} all-reduce(f32[512,8]{0,1:T(8,128)S(1)} %stack.67), channel_id=1, replica_groups=mesh['groups'=2,'seq'=4,'slide'=2,'head'=2] {'seq'}, use_global_device_ids=true, to_apply=%region_8.9 | all-reduce | flops 4096 | bytes 32768 | tf_op jit(solution)/shard_map/pmax | solution.py:47
  51.6 2.0 %convolution_dynamic-update-slice_fusion.7 = f32[512,512]{0,1:T(8,128)} fusion(f32[512,256]{0,1:T(8,128)} %get-tuple-element.51, f32[512]{0:T(512)S(1)} %bitcast.207, pred[256]{0:T(512)(128)(4,1)S(1)} %broadcast_bitcast_fusion, bf16[256,512]{1,0:T(8,128)(2,1)} %bitcast.163), kind=kOutput, calls=%fused_computation.57 | convolution fusion | flops 17170432 | bytes 723200 | tf_op jit(solution)/shard_map/dot_general | solution.py:61
  53.6 0.9 convolution_dynamic-update-slice_fusion.6
  54.7 0.9 convolution_dynamic-update-slice_fusion.5
  55.6 0.9 convolution_dynamic-update-slice_fusion.4
  56.6 0.9 convolution_dynamic-update-slice_fusion.3
  57.5 0.9 convolution_dynamic-update-slice_fusion.2
  58.5 0.9 convolution_dynamic-update-slice_fusion.1
  59.4 0.9 convolution_dynamic-update-slice_fusion
  60.4 2.5 %fusion.97 = (f32[512]{0:T(512)S(1)}, f32[512]{0:T(512)S(1)}, f32[512]{0:T(512)S(1)}, f32[512]{0:T(512)S(1)}, f32[512]{0:T(512)S(1)}, /*index=5*/f32[512]{0:T(512)S(1)}, f32[512]{0:T(512)S(1)}, f32[512]{0:T(512)S(1)}) fusion(f32[512,256]{0,1:T(8,128)S(1)} %get-tuple-element.65, f32[512]{0:T(512)S(1)} %bitcast.184, ...), kind=kLoop, calls=%fused_computation.158 | loop fusion | flops 3141632 | bytes 4227328 | tf_op jit(solution)/shard_map/reduce_sum | solution.py:59
  63.5 1.4 fusion.32
  64.9 21.1 %all_gather.13 = bf16[512,512]{0,1:T(8,128)(2,1)S(1)} all-gather(bf16[128,512]{0,1:T(8,128)(2,1)S(1)} %fusion.32), channel_id=1, replica_groups=mesh['groups'=2,'seq'=4,'slide'=2,'head'=2] {'seq'}, dimensions={0}, use_global_device_ids=true | all-gather | bytes 655360 | tf_op jit(solution)/shard_map/all_gather | solution.py:85
  86.0 19.5 %psum.15 = f32[512,8]{0,1:T(8,128)S(1)} all-reduce(f32[512,8]{0,1:T(8,128)S(1)} %stack.76), channel_id=1, replica_groups=mesh['groups'=2,'seq'=4,'slide'=2,'head'=2] {'seq'}, use_global_device_ids=true, to_apply=%region_18.19 | all-reduce | flops 4096 | bytes 32768 | tf_op jit(solution)/shard_map/psum | solution.py:69
  105.6 2.0 %fusion.42 = bf16[1,256,512]{1,2,0:T(8,128)(2,1)} fusion(bf16[512,512]{0,1:T(8,128)(2,1)S(1)} %all_gather.13, f32[512,256]{0,1:T(8,128)} %get-tuple-element.51, f32[512]{0:T(512)S(1)} %bitcast.233, f32[512]{0:T(512)S(1)} %bitcast.209, pred[256]{0:T(512)(128)(4,1)S(1)} %broadcast_bitcast_fusion), kind=kOutput, calls=%fused_computation.92 | convolution fusion | flops 17317888 | bytes 627200 | tf_op jit(solution)/shard_map/qt,qc->tc/dot_general | solution.py:100
  114.5 1.8 %copy.44 = bf16[1,256,512]{2,1,0:T(8,128)(2,1)} copy(bf16[1,256,512]{1,2,0:T(8,128)(2,1)} %fusion.56) | data formatting | bytes 524288
  116.3 2.3 %bitcast_reduce_fusion = (f32[512,8]{0,1:T(8,128)S(1)}, bf16[512,512]{0,1:T(8,128)(2,1)}) fusion(bf16[512,512]{0,1:T(8,128)(2,1)S(1)} %all_gather.13, f32[512,512]{0,1:T(8,128)} %all-reduce.2.cloned.1.call-done, f32[512,8]{0,1:T(8,128)S(1)} %psum.15, pred[512]{0:T(512)(128)(4,1)S(1)} %iota_compare_fusion), kind=kLoop, calls=%fused_computation.123 | loop fusion | flops 1830912 | bytes 2130432 | tf_op jit(solution)/shard_map/reduce_sum | solution.py:86
  125.6 0.9 fusion.60
  126.6 0.9 fusion.39
  128.3 0.9 fusion.37
  130.0 0.9 fusion.35
  131.8 0.9 fusion.33
  132.7 2.0 %copy.54 = bf16[512,512]{1,0:T(8,128)(2,1)} copy(bf16[512,512]{0,1:T(8,128)(2,1)} %fusion.33) | data formatting | bytes 1048576
  138.1 1.9 %convolution_convert_fusion = bf16[128,1024]{1,0:T(8,128)(2,1)} fusion(bf16[512,1024]{1,0:T(8,128)(2,1)S(1)} %copy-done, bf16[512,512]{0,1:T(8,128)(2,1)} %get-tuple-element.25, s32[]{:T(128)S(6)} %select_n.77), kind=kOutput, calls=%fused_computation.48 | convolution fusion | flops 134348800 | bytes 1441796 | tf_op jit(solution)/shard_map/dot_general | solution.py:77
  141.4 14.4 %reduce-scatter.7.cloned.1.call-done = bf16[128,512]{1,0:T(8,128)(2,1)} async-done(((bf16[512,512]{1,0:T(8,128)(2,1)}), bf16[128,512]{1,0:T(8,128)(2,1)}) %reduce-scatter.7.cloned.1.call-update) | async-done | bytes 131088
  155.9 1.0 copy.55
  156.9 5.7 %all-gather = bf16[256,512]{0,1:T(8,128)(2,1)S(1)} all-gather(bf16[128,512]{0,1:T(8,128)(2,1)S(1)} %copy.55), channel_id=2, replica_groups=mesh['groups'=2,'seq'=4,'slide'=2,'head'=2] {'slide'}, dimensions={0}, use_global_device_ids=true | all-gather | bytes 393216 | tf_op jit(solution)/shard_map/all_gather | solution.py:12
  (110 shorter events, 25.3 us)
Async XLA Ops:
  7.2 56.4 %copy-start = (bf16[512,1024]{1,0:T(8,128)(2,1)S(1)}, bf16[512,1024]{1,0:T(8,128)(2,1)}, u32[]{:S(2)}) copy-start(bf16[512,1024]{1,0:T(8,128)(2,1)} %param.12) | copy-start | bytes 3145732
  7.2 109.1 %all-reduce.2.cloned.1.call-start = ((), (), s32[]{:S(2)}) async-start(), calls=%async_computation.2 | async-start | bytes 2097152 | tf_op jit(solution)/shard_map/psum | solution.py:69
  8.0 17.7 %copy-start.24 = (bf16[1,256,512]{2,1,0:T(8,128)(2,1)S(1)}, bf16[1,256,512]{2,1,0:T(8,128)(2,1)}, u32[]{:S(2)}) copy-start(bf16[1,256,512]{2,1,0:T(8,128)(2,1)} %param.8) | copy-start | bytes 786436
  26.6 33.7 %copy-start.1 = (f32[512,256]{0,1:T(8,128)}, f32[512,256]{0,1:T(8,128)S(1)}, u32[]{:S(2)}) copy-start(f32[512,256]{0,1:T(8,128)S(1)} %get-tuple-element.61) | copy-start | bytes 1572868
  51.6 2.1 %copy-start.13 = (f32[512,256]{0,1:T(8,128)S(1)}, f32[512,256]{0,1:T(8,128)}, u32[]{:S(2)}) copy-start(f32[512,256]{0,1:T(8,128)} %get-tuple-element.53) | copy-start | bytes 1572868
  51.6 2.0 %copy-start.26 = (bf16[1,256,512]{2,1,0:T(8,128)(2,1)S(1)}, bf16[1,256,512]{2,1,0:T(8,128)(2,1)}, u32[]{:S(2)}) copy-start(bf16[1,256,512]{2,1,0:T(8,128)(2,1)} %param.9) | copy-start | bytes 786436
  53.6 1.0 copy-start.10
  54.6 1.1 copy-start.7
  55.6 1.1 copy-start.4
  60.3 95.6 %reduce-scatter.7.cloned.1.call-start = ((), (), s32[]{:S(2)}) async-start(), calls=%async_computation.4 | async-start | bytes 655360
  105.6 2.0 %copy-start.14 = (f32[512,256]{0,1:T(8,128)S(1)}, f32[512,256]{0,1:T(8,128)}, u32[]{:S(2)}) copy-start(f32[512,256]{0,1:T(8,128)} %get-tuple-element.53) | copy-start | bytes 1572868
  107.6 1.0 copy-start.11
  108.7 1.0 copy-start.8
  109.7 1.0 copy-start.5
  110.8 1.0 copy-start.2
  116.3 2.4 %copy-start.27 = (bf16[1,256,512]{2,1,0:T(8,128)(2,1)S(1)}, bf16[1,256,512]{2,1,0:T(8,128)(2,1)}, u32[]{:S(2)}) copy-start(bf16[1,256,512]{2,1,0:T(8,128)(2,1)} %param.9) | copy-start | bytes 786436
  116.3 2.4 %copy-start.28 = (f32[512,256]{0,1:T(8,128)S(1)}, f32[512,256]{0,1:T(8,128)}, u32[]{:S(2)}) copy-start(f32[512,256]{0,1:T(8,128)} %get-tuple-element.51) | copy-start | bytes 1572868
  118.9 1.7 copy-start.15
  120.6 1.0 copy-start.12
  121.6 1.0 copy-start.9
  121.9 5.6 %copy-start.16 = (bf16[512,256]{0,1:T(8,128)(2,1)}, bf16[512,256]{0,1:T(8,128)(2,1)S(1)}, u32[]{:S(2)}) copy-start(bf16[512,256]{0,1:T(8,128)(2,1)S(1)} %fusion.29) | copy-start | bytes 786436
  122.7 1.0 copy-start.6
  123.0 5.3 %copy-start.18 = (bf16[512,256]{0,1:T(8,128)(2,1)}, bf16[512,256]{0,1:T(8,128)(2,1)S(1)}, u32[]{:S(2)}) copy-start(bf16[512,256]{0,1:T(8,128)(2,1)S(1)} %fusion.28) | copy-start | bytes 786436
  123.7 1.0 copy-start.3
  124.0 5.2 %copy-start.20 = (bf16[512,256]{0,1:T(8,128)(2,1)}, bf16[512,256]{0,1:T(8,128)(2,1)S(1)}, u32[]{:S(2)}) copy-start(bf16[512,256]{0,1:T(8,128)(2,1)S(1)} %fusion.27) | copy-start | bytes 786436
  125.1 5.0 %copy-start.22 = (bf16[512,256]{0,1:T(8,128)(2,1)}, bf16[512,256]{0,1:T(8,128)(2,1)S(1)}, u32[]{:S(2)}) copy-start(bf16[512,256]{0,1:T(8,128)(2,1)S(1)} %fusion.26) | copy-start | bytes 786436
  125.6 1.0 copy-start.25
  134.7 0.9 copy-start.17
  134.7 1.0 copy-start.29
  134.7 1.2 copy-start.19
  134.7 30.0 %reduce-scatter.5.cloned.1.call-start = ((), (), s32[]{:S(2)}) async-start(), calls=%async_computation.3 | async-start | bytes 393216 | tf_op jit(solution)/shard_map/reduce_scatter | solution.py:79
  135.9 1.0 copy-start.21
  (1 other events, 0.9 us)
Sparse Core Ops, SparseCore 0:
  60.4 55.6 all-reduce.1
  134.9 20.9 reduce-scatter.6
  158.7 5.9 reduce-scatter.4
